TPU v7x, 32 devices: a whole 2x2x4 slice. The times are simulated.
32 devices in a mesh: sweep: 2 (over x), expert: 4 (over y, core), fsdp: 4 (over z).
Axes of the slice: x: 2, y: 2, z: 4, core: 2. Of those that a mesh axis runs over, the one named last changes fastest.
Arguments:
- tokens: bfloat16 [4096, 2048], P(('sweep', 'expert', 'fsdp')), parts along dimension 0, may hold values from -6 to 6
- context: bfloat16 [4096, 2048], P(('sweep', 'expert', 'fsdp')), parts along dimension 0, may hold values from -6 to 6
- out_proj: bfloat16 [4096, 2048], P(('sweep', 'expert', 'fsdp')), parts along dimension 0, may hold values from -0.125 to 0.125
- norm_gain: float32 [4096], P('sweep'), parts along dimension 0, may hold values from 0.1 to 1.9
- router: bfloat16 [4096, 8], P('sweep'), parts along dimension 0, may hold values from -0.125 to 0.125
- expert_ids: int32 [4096, 2], P(('sweep', 'expert', 'fsdp')), parts along dimension 0, may hold values from 0 to 7, all different within a row; in each aligned block of 128 rows (0 to 127, 128 to 255, ...) at most 40 rows name the same one
- w_gate_up: bfloat16 [32, 2, 704, 2048], P(('sweep', 'expert', 'fsdp')), parts along dimension 0, may hold values from -0.125 to 0.125
- w_down: bfloat16 [32, 704, 2048], P(('sweep', 'expert', 'fsdp')), parts along dimension 0, may hold values from -0.15625 to 0.15625
Outputs:
- layer_out: bfloat16 [4096, 2048], P(('sweep', 'expert', 'fsdp')), parts along dimension 0
There are 2 independent parts, one for each index of `sweep`. A program takes and returns all parts, laid end to end along the dimension named above; each array names one. Nothing has to cross between parts.
Inputs may be any that keep to these rules, and one draw needn't show every extreme that they name: `expert_ids`: each row names two different experts. Among the rows of one device no expert is named more than 40 times, a bound that some block reaches.
All inputs are finite; a program needn't handle non-finite values.
Results may differ from a plain program's by a relative error of at most 0.012.
Values may be sent and summed in bfloat16 or wider, within the bound.
A program may use at most 64 MiB of HBM per device.

v0:
```python
import functools

import jax
import jax.numpy as jnp
from jax import lax
from jax.experimental import pallas as pl
from jax.experimental.pallas import tpu as pltpu
from jax.sharding import PartitionSpec as P

eps_norm = 1e-05
MESH = pl.DeviceIdType.MESH
VMEM_GRANT = 60 * 1024 * 1024


def both(a, b):
    return jnp.logical_and(a, b)


def inside(i, n):
    return both(i >= 0, i < n)


def block_kernel(
    columns, members, cap, slots,
    tok, ctx, wout, gain, router, ids, gu_hbm, dn_hbm,
    out,
    gath, acc, gu, dn, outbox, inbox, part, partner, ret, resid,
    load_sem, ag_send, ag_recv, disp_send, disp_recv, fwd_send,
    part_send, part_recv, ret_send, ret_recv,
):
    n = columns * members
    lines = columns // 2
    pairs = members // 2
    experts = columns * pairs
    rows, width = tok.shape
    k_rows = wout.shape[0]
    my_e = lax.axis_index("expert")
    my_f = lax.axis_index("fsdp")
    me = my_e * members + my_f
    my_y, my_c = lax.div(my_e, 2), lax.rem(my_e, 2)
    my_p = lax.div(my_f, 2)
    my_expert = my_e * pairs + my_p

    def dev(e, f):
        return {"expert": e, "fsdp": f}

    load_gu = pltpu.make_async_copy(gu_hbm.at[0], gu, load_sem.at[0])
    load_dn = pltpu.make_async_copy(dn_hbm.at[0], dn, load_sem.at[1])
    load_gu.start()
    load_dn.start()

    barrier = pltpu.get_barrier_semaphore()

    def greet(i, _):
        other = lax.rem(me + i, n)
        pl.semaphore_signal(
            barrier, inc=1, device_id=dev(lax.div(other, members), lax.rem(other, members)),
            device_id_type=MESH)
        return 0

    lax.fori_loop(1, n, greet, 0)
    pl.semaphore_wait(barrier, n - 1)

    def place(e, f):
        return pl.ds(pl.multiple_of((e * members + f) * k_rows, k_rows), k_rows)

    def ag(e, f, way, target, own=False):
        b = e * members + f
        return pltpu.make_async_remote_copy(
            src_ref=wout if own else gath.at[place(e, f)],
            dst_ref=gath.at[place(e, f)],
            send_sem=ag_send.at[b, way],
            recv_sem=ag_recv.at[b],
            device_id=target,
            device_id_type=MESH)

    def ag_arrived(e, f):
        ag(e, f, 0, dev(my_y * 2 + 1 - my_c, my_f)).wait_recv()

    def z_copies(s, sign):
        fb, to = my_f + sign * s, my_f - sign
        k = 0 if sign == 1 else 1
        own = s == 0
        result = [(inside(to, members), lambda: ag(my_e, fb, k, dev(my_e, jnp.clip(to, 0, members - 1)), own))]
        if s > 0 or sign == 1:
            for j, ysign in enumerate((1, -1)):
                yt = my_y - ysign
                result.append((
                    inside(yt, lines),
                    lambda yt=yt, j=j: ag(my_e, fb, 2 + j, dev(jnp.clip(yt, 0, lines - 1) * 2 + my_c, my_f), own)))
            result.append((None, lambda: ag(my_e, fb, 4, dev(my_y * 2 + 1 - my_c, my_f), own)))
        return inside(fb, members), fb, result

    def y_copies(t, s, sign, ysign):
        fb = my_f + sign * s
        yb, yt = my_y + ysign * t, my_y - ysign
        e_b = yb * 2 + my_c
        j = 0 if ysign == 1 else 1
        result = []
        if t < lines - 1:
            result.append((
                inside(yt, lines),
                lambda: ag(e_b, fb, 2 + j, dev(jnp.clip(yt, 0, lines - 1) * 2 + my_c, my_f))))
        result.append((None, lambda: ag(e_b, fb, 4, dev(my_y * 2 + 1 - my_c, my_f))))
        return both(inside(fb, members), inside(yb, lines)), e_b, fb, result

    def apply(result, finish):
        for cond, make in result:
            def go(make=make):
                if finish:
                    make().wait_send()
                else:
                    make().start()
            if cond is None:
                go()
            else:
                pl.when(cond)(go)

    def z_step(s, finish=False):
        for sign in (1, -1):
            ok, fb, result = z_copies(s, sign)

            @pl.when(ok)
            def _():
                if s > 0 and not finish:
                    ag_arrived(my_e, fb)
                apply(result, finish)

    def y_step(t, s, finish=False):
        for ysign in (1, -1):
            for sign in (1, -1) if s else (1,):
                ok, e_b, fb, result = y_copies(t, s, sign, ysign)

                @pl.when(ok)
                def _():
                    if not finish:
                        ag_arrived(e_b, fb)
                    apply(result, finish)

    depth = members * k_rows
    col = min(512, width)

    def multiply(e):
        at = pl.ds(pl.multiple_of(e * depth, depth), depth)
        a = ctx[:, at]

        def one(i, _):
            cols = pl.ds(pl.multiple_of(i * col, col), col)
            acc[:, cols] += jnp.dot(a, gath[at, cols], preferred_element_type=jnp.float32)
            return 0

        lax.fori_loop(0, width // col, one, 0)

    z_step(0)
    gath[place(my_e, my_f), :] = wout[...]
    acc[...] = tok[...].astype(jnp.float32)
    for s in range(1, members):
        z_step(s)
        if lines > 1:
            y_step(1, s - 1)
    multiply(my_e)
    if lines > 1:
        y_step(1, members - 1)
        for t in range(2, lines):
            for s in range(members):
                y_step(t, s)

    diagonal = jnp.where(
        lax.broadcasted_iota(jnp.int32, (rows, rows), 0) == lax.broadcasted_iota(jnp.int32, (rows, rows), 1), 1.0, 0.0)
    named_ids = ids[...].astype(jnp.float32)
    id0 = jnp.sum(diagonal * named_ids[0:1], axis=1, keepdims=True).astype(jnp.int32)
    id1 = jnp.sum(diagonal * named_ids[1:2], axis=1, keepdims=True).astype(jnp.int32)
    named = lax.broadcasted_iota(jnp.int32, (rows, experts), 1)
    hot0 = jnp.where(named == id0, 1.0, 0.0)
    hot1 = jnp.where(named == id1, 1.0, 0.0)
    earlier = jnp.where(
        lax.broadcasted_iota(jnp.int32, (rows, rows), 1) < lax.broadcasted_iota(jnp.int32, (rows, rows), 0),
        1.0, 0.0).astype(jnp.bfloat16)
    before = jnp.dot(earlier, (hot0 + hot1).astype(jnp.bfloat16), preferred_element_type=jnp.float32)
    slot0 = id0 * slots + jnp.sum(before * hot0, axis=1, keepdims=True).astype(jnp.int32)
    slot1 = id1 * slots + jnp.sum(before * hot1, axis=1, keepdims=True).astype(jnp.int32)
    slot_no = lax.broadcasted_iota(jnp.int32, (rows, experts * slots), 1)
    at0, at1 = slot_no == slot0, slot_no == slot1
    send_mask = jnp.where(jnp.logical_or(at0, at1), 1.0, 0.0).astype(jnp.bfloat16)

    def other_lines(t, _):
        multiply(lax.rem(my_y + t, lines) * 2 + my_c)
        return 0

    lax.fori_loop(1, lines, other_lines, 0)

    def other_core(t, _):
        e = lax.rem(my_y + t, lines) * 2 + 1 - my_c

        def one(f, _):
            ag_arrived(e, f)
            return 0

        lax.fori_loop(0, members, one, 0)
        multiply(e)
        return 0

    lax.fori_loop(0, lines, other_core, 0)

    rounded = acc[...].astype(jnp.bfloat16)
    resid[...] = rounded
    widened = rounded.astype(jnp.float32)
    inv = lax.rsqrt(jnp.mean(widened * widened, axis=1, keepdims=True) + eps_norm)
    normed = (widened * inv * gain[...]).astype(jnp.bfloat16)
    boxes = lax.dot_general(
        send_mask, normed, (((0,), (0,)), ((), ())), preferred_element_type=jnp.float32
    ).astype(jnp.bfloat16)
    for e in range(experts):
        outbox[e] = boxes[e * slots:(e + 1) * slots]

    def near_of(f, p):
        return jnp.clip(f, 2 * p, 2 * p + 1)

    def dispatch(e, p):
        x = e * pairs + p
        return pltpu.make_async_remote_copy(
            src_ref=outbox.at[x], dst_ref=inbox.at[me],
            send_sem=disp_send.at[x], recv_sem=disp_recv.at[me],
            device_id=dev(e, near_of(my_f, p)), device_id_type=MESH)

    def each_target(finish):
        for q in range(pairs):
            p = lax.rem(my_p + q, pairs)

            def one(i, _):
                e = lax.rem(my_e + i, columns)
                if finish:
                    dispatch(e, p).wait_send()
                else:
                    dispatch(e, p).start()
                return 0

            lax.fori_loop(0 if q else 1, columns, one, 0)

    each_target(False)
    inbox[me] = outbox[my_expert]

    far_f = 4 * my_p + 1 - my_f

    def forward(b):
        return pltpu.make_async_remote_copy(
            src_ref=inbox.at[b], dst_ref=inbox.at[b],
            send_sem=fwd_send.at[b], recv_sem=disp_recv.at[b],
            device_id=dev(my_e, far_f), device_id_type=MESH)

    upper = 4 * my_p >= members

    def group_of(g):
        k = jnp.where(g < 2, 1 - g, g)
        return lax.rem(jnp.where(upper, 2 * my_p + 1 - k, 2 * my_p + k) + members, members)

    def i_am_near(fs):
        return near_of(fs, my_p) == my_f

    def box_of(fs, i):
        return lax.rem(my_e + i, columns) * members + fs

    def pass_on(k):
        fs = jnp.where(lax.rem(my_f, 2) == 1, my_f + k, my_f - k)

        @pl.when(inside(fs, members))
        def _():
            def one(i, _):
                b = box_of(fs, i)

                @pl.when(b != me)
                def _():
                    forward(b).wait_recv()

                forward(b).start()
                return 0

            lax.fori_loop(0, columns, one, 0)

    def passed_here(fs):
        @pl.when(jnp.logical_not(i_am_near(fs)))
        def _():
            def one(i, _):
                forward(box_of(fs, i)).wait_recv()
                return 0

            lax.fori_loop(0, columns, one, 0)

    def give(b):
        return pltpu.make_async_remote_copy(
            src_ref=part.at[b], dst_ref=partner.at[b],
            send_sem=part_send.at[b], recv_sem=part_recv.at[b],
            device_id=dev(my_e, far_f), device_id_type=MESH)

    def give_back(b):
        return pltpu.make_async_remote_copy(
            src_ref=part.at[b], dst_ref=ret.at[my_expert],
            send_sem=ret_send.at[b], recv_sem=ret_recv.at[my_expert],
            device_id=dev(lax.div(b, members), lax.rem(b, members)), device_id_type=MESH)

    nt = (((1,), (1,)), ((), ()))

    def expert(g):
        fs = group_of(g)
        passed_here(fs)
        x = jnp.concatenate([inbox[e * members + fs] for e in range(columns)], axis=0)
        gate = lax.dot_general(x, gu[0], nt, preferred_element_type=jnp.float32)
        up = lax.dot_general(x, gu[1], nt, preferred_element_type=jnp.float32)
        hidden = (gate / (1.0 + jnp.exp(-gate)) * up).astype(jnp.bfloat16)
        piece = jnp.dot(hidden, dn[...], preferred_element_type=jnp.float32).astype(jnp.bfloat16)
        for e in range(columns):
            part[e * members + fs] = piece[e * slots:(e + 1) * slots]

        @pl.when(jnp.logical_not(i_am_near(fs)))
        def _():
            def one(i, _):
                give(box_of(fs, i)).start()
                return 0

            lax.fori_loop(0, columns, one, 0)

    def finish_group(g):
        fs = group_of(g)

        @pl.when(i_am_near(fs))
        def _():
            def one(i, _):
                b = box_of(fs, i)
                give(b).wait_recv()
                part[b] = (part[b].astype(jnp.float32) + partner[b].astype(jnp.float32)).astype(jnp.bfloat16)

                @pl.when(b == me)
                def _():
                    ret[my_expert] = part[b]

                @pl.when(b != me)
                def _():
                    give_back(b).start()
                return 0

            lax.fori_loop(0, columns, one, 0)

    logits = lax.dot_general(normed, router[...], nt, preferred_element_type=jnp.float32)
    s0 = jax.nn.sigmoid(jnp.sum(logits * hot0, axis=1, keepdims=True))
    s1 = jax.nn.sigmoid(jnp.sum(logits * hot1, axis=1, keepdims=True))
    total = s0 + s1
    weights = jnp.where(at0, s0 / total, 0.0) + jnp.where(at1, s1 / total, 0.0)
    weights_high = weights.astype(jnp.bfloat16)
    weights_low = (weights - weights_high.astype(jnp.float32)).astype(jnp.bfloat16)

    load_gu.wait()
    load_dn.wait()

    pass_on(0)

    def step(g, _):
        @pl.when(g + 1 < members)
        def _():
            pass_on(g + 1)

        expert(g)

        @pl.when(g > 0)
        def _():
            finish_group(g - 1)
        return 0

    lax.fori_loop(0, members, step, 0)
    finish_group(members - 1)

    def came_back(x, _):
        @pl.when(x != my_expert)
        def _():
            pltpu.make_async_remote_copy(
                src_ref=ret.at[x], dst_ref=ret.at[x],
                send_sem=disp_send.at[x], recv_sem=ret_recv.at[x],
                device_id=dev(my_e, far_f), device_id_type=MESH).wait_recv()
        return 0

    lax.fori_loop(0, experts, came_back, 0)
    results = jnp.concatenate([ret[x] for x in range(experts)], axis=0)
    mixed = jnp.dot(weights_high, results, preferred_element_type=jnp.float32)
    mixed = mixed + jnp.dot(weights_low, results, preferred_element_type=jnp.float32)
    out[...] = (resid[...].astype(jnp.float32) + mixed).astype(jnp.bfloat16)

    for s in range(members):
        z_step(s, True)
        for t in range(1, lines):
            y_step(t, s, True)
    each_target(True)

    def drain(b, _):
        fs = lax.rem(b, members)
        mine = lax.div(b, members)

        @pl.when(i_am_near(fs))
        def _():
            forward(b).wait_send()

            @pl.when(b != me)
            def _():
                give_back(b).wait_send()

        @pl.when(jnp.logical_not(i_am_near(fs)))
        def _():
            give(b).wait_send()
        return 0

    lax.fori_loop(0, n, drain, 0)


def on_device(tokens, context, out_proj, norm_gain, router, expert_ids, w_gate_up, w_down):
    rows, width = tokens.shape
    columns = lax.axis_size("expert")
    members = lax.axis_size("fsdp")
    n = columns * members
    experts = n // 2
    cap = 5 * rows // (2 * experts)
    slots = -(-cap // 8) * 8
    units = w_down.shape[1]
    vmem = pl.BlockSpec(memory_space=pltpu.VMEM)
    far = pl.BlockSpec(memory_space=pl.ANY)
    bf = jnp.bfloat16
    dma = pltpu.SemaphoreType.DMA
    call = pl.pallas_call(
        functools.partial(block_kernel, columns, members, cap, slots),
        out_shape=jax.ShapeDtypeStruct((rows, width), bf),
        in_specs=[vmem] * 6 + [far] * 2,
        out_specs=vmem,
        scratch_shapes=[
            pltpu.VMEM((n * out_proj.shape[0], width), bf),
            pltpu.VMEM((rows, width), jnp.float32),
            pltpu.VMEM((2, units, width), bf),
            pltpu.VMEM((units, width), bf),
            pltpu.VMEM((experts, slots, width), bf),
            pltpu.VMEM((n, slots, width), bf),
            pltpu.VMEM((n, slots, width), bf),
            pltpu.VMEM((n, slots, width), bf),
            pltpu.VMEM((experts, slots, width), bf),
            pltpu.VMEM((rows, width), bf),
            dma((2,)), dma((n, 5)), dma((n,)), dma((experts,)), dma((n,)), dma((n,)),
            dma((n,)), dma((n,)), dma((n,)), dma((experts,)),
        ],
        compiler_params=pltpu.CompilerParams(
            collective_id=0, has_side_effects=True, vmem_limit_bytes=VMEM_GRANT),
    )
    return call(tokens, context, out_proj, norm_gain.reshape(1, width), router.T, expert_ids.T, w_gate_up, w_down)


def solution(mesh):
    group = ("sweep", "expert", "fsdp")
    return jax.shard_map(
        on_device,
        mesh=mesh,
        in_specs=(
            P(group, None), P(group, None), P(group, None), P("sweep"), P("sweep", None),
            P(group, None), P(group, None, None, None), P(group, None, None),
        ),
        out_specs=P(group, None),
        check_vma=False,
    )
```

profile of v0, /device:TPU:0, one launch (start us, length us, event | category | flops | bytes accessed | tf_op | source)
XLA Modules:
  0.0 158.3 jit_solution(7698434091408725219)
XLA Ops:
  0.0 156.4 %shard_map.82 = bf16[128,2048]{1,0:T(8,128)(2,1)} custom-call(bf16[128,2048]{1,0:T(8,128)(2,1)} %tok.1, bf16[128,2048]{1,0:T(8,128)(2,1)} %ctx.1, bf16[128,2048]{1,0:T(8,128)(2,1)} %wout.1, f32[1,2048]{1,0:T(1,128)} %bitcast.4, bf16[8,2048]{1,0:T(8,128)(2,1)} %bitcast.3, s32[2,128]{1,0:T(2,128)} %bitcast.5, bf16[1,2,704,2048]{3,2,1,0:T(8,128)(2,1)} %gu_hbm.1, ...), custom_call_target="tpu_custom_call" | custom-call | tf_op jit(solution)/shard_map/pallas_call | solution.py:447
  156.4 1.9 %copy.10 = bf16[128,2048]{1,0:T(8,128)(2,1)} copy(bf16[128,2048]{1,0:T(8,128)(2,1)} %shard_map.82) | data formatting | bytes 1048576
where the time goes:
time: 159 us; the launch traced here: 158 us
  Pallas kernels  156 us (98%)
  local copies, waits for them, and re-layouts  1.88 us (1%)
    pallas_call x1, Pallas kernels, on_device(): call(tokens, context, out_proj, norm_gain.reshape(1, width), router.T, ex...  156 us

commit v1 on v0

v1 whole, which is shorter than its diff:
```python
import functools

import jax
import jax.numpy as jnp
from jax import lax
from jax.experimental import pallas as pl
from jax.experimental.pallas import tpu as pltpu
from jax.sharding import PartitionSpec as P

eps_norm = 1e-05
MESH = pl.DeviceIdType.MESH
VMEM_GRANT = 62 * 1024 * 1024
NT = (((1,), (1,)), ((), ()))
TN = (((0,), (0,)), ((), ()))


def both(a, b):
    return jnp.logical_and(a, b)


def inside(i, n):
    return both(i >= 0, i < n)


def block_kernel(
    columns, members, slots, col,
    tok, ctx, wout, gain, router, ids, gu_hbm, dn_hbm,
    out,
    gath, ctxs, acc, pout, pin, gu, dn, resid,
    idsb, hot, mask, gates, tokb, outb, inb, hid, part, back, total, rs_out, rs_in,
    load_sem, w_send, w_recv, id_send, id_recv, c_send, c_recv, p_send, p_recv,
    t_send, t_recv, b_send, b_recv, r_send, r_recv, s_send, s_recv,
):
    lines = columns // 2
    pairs = members // 2
    experts = columns * pairs
    rows, width = tok.shape
    k_rows = wout.shape[0]
    depth = 2 * members * k_rows
    chunks = width // col
    my_e = lax.axis_index("expert")
    my_f = lax.axis_index("fsdp")
    my_y, my_c = lax.div(my_e, 2), lax.rem(my_e, 2)
    my_p = lax.div(my_f, 2)
    other = my_y * 2 + 1 - my_c

    def dev(e, f):
        return {"expert": e, "fsdp": f}

    def span(j):
        return pl.ds(pl.multiple_of(j * col, col), col)

    def copy(src, dst, send, recv, target):
        return pltpu.make_async_remote_copy(
            src_ref=src, dst_ref=dst, send_sem=send, recv_sem=recv,
            device_id=target, device_id_type=MESH)

    def loop(lo, hi, body):
        def one(i, _):
            body(i)
            return 0

        lax.fori_loop(lo, hi, one, 0)

    load_gu = pltpu.make_async_copy(gu_hbm.at[0], gu, load_sem.at[0])
    load_dn = pltpu.make_async_copy(dn_hbm.at[0], dn, load_sem.at[1])

    barrier = pltpu.get_barrier_semaphore()

    def greet(e, f):
        pl.semaphore_signal(barrier, inc=1, device_id=dev(e, f), device_id_type=MESH)

    for sign in (1, -1):
        @pl.when(inside(my_f + sign, members))
        def _():
            greet(my_e, my_f + sign)

    loop(1, columns, lambda i: greet(lax.rem(my_e + i, columns), my_f))
    beside = jnp.where(my_f > 0, 1, 0) + jnp.where(my_f < members - 1, 1, 0)
    pl.semaphore_wait(barrier, columns - 1 + beside)

    def place(c, f):
        return pl.ds(pl.multiple_of((c * members + f) * k_rows, k_rows), k_rows)

    def w_copy(f, j, way, target, own=False):
        at = gath.at[place(my_c, f), span(j)]
        return copy(wout.at[:, span(j)] if own else at, at,
                    w_send.at[f, j, way], w_recv.at[my_c, f, j], target)

    def w_arrived(c, f, j):
        at = gath.at[place(c, f), span(j)]
        copy(at, at, w_send.at[f, j, 0], w_recv.at[c, f, j], dev(other, my_f)).wait_recv()

    def id_copy(f, way, target, own=False):
        return copy(ids if own else idsb.at[f], idsb.at[f], id_send.at[f, way], id_recv.at[f], target)

    def ctx_copy(r):
        line = lax.rem(my_y + r, lines)
        at = pl.ds(pl.multiple_of(line * depth, depth), depth)
        return copy(ctx.at[:, at], ctxs.at[lines - r], c_send.at[r], c_recv.at[lines - r],
                    dev(line * 2 + my_c, my_f))

    def w_start(j, finish):
        for way, sign in ((0, 1), (1, -1)):
            to = my_f + sign

            @pl.when(inside(to, members))
            def _():
                mine = w_copy(my_f, j, way, dev(my_e, to), True)
                mine.wait_send() if finish else mine.start()
        mine = w_copy(my_f, j, 2, dev(other, my_f), True)
        mine.wait_send() if finish else mine.start()

    def id_start(finish):
        for way, sign in ((0, 1), (1, -1)):
            to = my_f + sign

            @pl.when(inside(to, members))
            def _():
                mine = id_copy(my_f, way, dev(my_e, to), True)
                mine.wait_send() if finish else mine.start()

    def w_step(s, j, finish=False):
        for way, sign in ((0, 1), (1, -1)):
            fb, to = my_f - sign * s, my_f + sign

            @pl.when(inside(fb, members))
            def _():
                if not finish:
                    w_arrived(my_c, fb, j)

                    @pl.when(j == 0)
                    def _():
                        id_copy(fb, way, dev(my_e, my_f)).wait_recv()

                @pl.when(inside(to, members))
                def _():
                    onward = w_copy(fb, j, way, dev(my_e, to))
                    onward.wait_send() if finish else onward.start()

                    @pl.when(j == 0)
                    def _():
                        named = id_copy(fb, way, dev(my_e, to))
                        named.wait_send() if finish else named.start()

                across = w_copy(fb, j, 2, dev(other, my_f))
                across.wait_send() if finish else across.start()

    loop(0, chunks, lambda j: w_start(j, False))
    id_start(False)
    for r in range(1, lines):
        ctx_copy(r).start()
    load_gu.start()
    load_dn.start()
    loop(0, chunks, lambda j: gath.__setitem__((place(my_c, my_f), span(j)), wout[:, span(j)]))
    idsb[my_f] = ids[...]
    ctxs[0] = ctx[:, pl.ds(pl.multiple_of(my_y * depth, depth), depth)]
    loop(0, (members - 2) * chunks, lambda i: w_step(1 + lax.div(i, chunks), lax.rem(i, chunks)))
    for r in range(1, lines):
        ctx_copy(r).wait_recv()

    def group_of(k):
        m = jnp.minimum(my_f, members - 1 - my_f)
        half = lax.div(k + 1, 2)
        near = jnp.where(lax.rem(k, 2) == 1, my_f - half, my_f + half)
        far = jnp.where(my_f > m, my_f - (k - m), my_f + (k - m))
        return jnp.where(k <= 2 * m, near, far)

    def make_masks(f):
        diagonal = jnp.where(
            lax.broadcasted_iota(jnp.int32, (rows, rows), 0) == lax.broadcasted_iota(jnp.int32, (rows, rows), 1),
            1.0, 0.0)
        names = idsb[f].astype(jnp.float32)
        id0 = jnp.sum(diagonal * names[0:1], axis=1, keepdims=True).astype(jnp.int32)
        id1 = jnp.sum(diagonal * names[1:2], axis=1, keepdims=True).astype(jnp.int32)
        every = lax.broadcasted_iota(jnp.int32, (rows, experts), 1)
        hot[f, 0] = jnp.where(every == id0, 1.0, 0.0)
        hot[f, 1] = jnp.where(every == id1, 1.0, 0.0)
        place_no = lax.broadcasted_iota(jnp.int32, (rows, columns), 1)
        here = place_no * pairs + my_p
        hot0 = jnp.where(here == id0, 1.0, 0.0)
        hot1 = jnp.where(here == id1, 1.0, 0.0)
        earlier = jnp.where(
            lax.broadcasted_iota(jnp.int32, (rows, rows), 1) < lax.broadcasted_iota(jnp.int32, (rows, rows), 0),
            1.0, 0.0).astype(jnp.bfloat16)
        before = jnp.dot(earlier, (hot0 + hot1).astype(jnp.bfloat16), preferred_element_type=jnp.float32)
        spot = before + (place_no * slots + 1).astype(jnp.float32)
        slot0 = jnp.sum(spot * hot0, axis=1, keepdims=True).astype(jnp.int32) - 1
        slot1 = jnp.sum(spot * hot1, axis=1, keepdims=True).astype(jnp.int32) - 1
        slot_no = lax.broadcasted_iota(jnp.int32, (rows, columns * slots), 1)
        mask[f, 0] = jnp.where(slot_no == slot0, 1.0, 0.0).astype(jnp.bfloat16)
        mask[f, 1] = jnp.where(slot_no == slot1, 1.0, 0.0).astype(jnp.bfloat16)

    def part_copy(r, j):
        line = lax.rem(my_y + r, lines)
        return copy(pout.at[r - 1, :, span(j)], pin.at[lines - r - 1, :, span(j)],
                    p_send.at[r - 1, j], p_recv.at[lines - r - 1, j], dev(line * 2 + my_c, my_f))

    def project(j):
        loop(lax.div(j * members, chunks), lax.div((j + 1) * members, chunks),
             lambda k: make_masks(group_of(k)))
        w_step(members - 1, j)
        loop(0, members, lambda f: w_arrived(1 - my_c, f, j))
        mixed = jnp.dot(ctxs[...].reshape(lines * rows, depth), gath[:, span(j)],
                        preferred_element_type=jnp.float32)
        for r in range(1, lines):
            pout[r - 1, :, span(j)] = mixed[r * rows:(r + 1) * rows].astype(jnp.bfloat16)
            part_copy(r, j).start()
        acc[:, span(j)] = mixed[:rows] + tok[:, span(j)].astype(jnp.float32)

    loop(0, chunks, project)

    if lines > 1:
        def add_parts(j):
            for r in range(1, lines):
                part_copy(r, j).wait_recv()
                acc[:, span(j)] += pin[lines - r - 1, :, span(j)].astype(jnp.float32)

        loop(0, chunks, add_parts)

    rounded = acc[...].astype(jnp.bfloat16)
    resid[...] = rounded
    widened = rounded.astype(jnp.float32)
    inv = lax.rsqrt(jnp.mean(widened * widened, axis=1, keepdims=True) + eps_norm)
    tokb[my_f] = (widened * inv * gain[...]).astype(jnp.bfloat16)

    def t_copy(f, j, way, target):
        at = tokb.at[f, :, span(j)]
        return copy(at, at, t_send.at[f, j, way], t_recv.at[f, j], target)

    def t_start(j, finish):
        for way, sign in ((0, 1), (1, -1)):
            to = my_f + sign

            @pl.when(inside(to, members))
            def _():
                mine = t_copy(my_f, j, way, dev(my_e, to))
                mine.wait_send() if finish else mine.start()

    def box_copy(f, e, j):
        return copy(outb.at[f, e, :, span(j)], inb.at[f, my_e, :, span(j)],
                    b_send.at[f, e], b_recv.at[f, my_e], dev(e, my_f))

    def box(f, j):
        boxed = lax.dot_general(mask[f, 0] + mask[f, 1], tokb[f, :, span(j)], TN,
                                preferred_element_type=jnp.float32).astype(jnp.bfloat16)
        for e in range(columns):
            outb[f, e, :, span(j)] = boxed[e * slots:(e + 1) * slots]
        loop(1, columns, lambda i: box_copy(f, lax.rem(my_e + i, columns), j).start())
        inb[f, my_e, :, span(j)] = outb[f, my_e, :, span(j)]

    def t_step(d, j, finish=False):
        for way, sign in ((0, 1), (1, -1)):
            fb, to = my_f - sign * d, my_f + sign

            @pl.when(inside(fb, members))
            def _():
                if not finish:
                    t_copy(fb, j, way, dev(my_e, my_f)).wait_recv()

                @pl.when(inside(to, members))
                def _():
                    onward = t_copy(fb, j, way, dev(my_e, to))
                    onward.wait_send() if finish else onward.start()

                if not finish:
                    box(fb, j)

    loop(0, chunks, lambda j: t_start(j, False))
    load_gu.wait()
    load_dn.wait()

    def back_copy(f, e, j):
        return copy(part.at[f, e, :, span(j)], back.at[f, my_e, :, span(j)],
                    r_send.at[f, e], r_recv.at[f, my_e, j], dev(e, my_f))

    def back_arrived(f, e, j):
        copy(part.at[f, e, :, span(j)], back.at[f, e, :, span(j)],
             r_send.at[f, e], r_recv.at[f, e, j], dev(e, my_f)).wait_recv()

    def expert(f):
        def boxes_arrived(i):
            e = lax.rem(my_e + i, columns)
            copy(outb.at[f, e], inb.at[f, e], b_send.at[f, e], b_recv.at[f, e], dev(e, my_f)).wait_recv()

        loop(1, columns, boxes_arrived)
        x = jnp.concatenate([inb[f, e] for e in range(columns)], axis=0)
        gate = lax.dot_general(x, gu[0], NT, preferred_element_type=jnp.float32)
        up = lax.dot_general(x, gu[1], NT, preferred_element_type=jnp.float32)
        hid[...] = (gate / (1.0 + jnp.exp(-gate)) * up).astype(jnp.bfloat16)

        def down(j):
            piece = jnp.dot(hid[...], dn[:, span(j)], preferred_element_type=jnp.float32).astype(jnp.bfloat16)
            for e in range(columns):
                part[f, e, :, span(j)] = piece[e * slots:(e + 1) * slots]
            loop(1, columns, lambda i: back_copy(f, lax.rem(my_e + i, columns), j).start())
            back[f, my_e, :, span(j)] = part[f, my_e, :, span(j)]

        loop(0, chunks, down)

        logits = lax.dot_general(tokb[f], router[...], NT, preferred_element_type=jnp.float32)
        s0 = jax.nn.sigmoid(jnp.sum(logits * hot[f, 0], axis=1, keepdims=True))
        s1 = jax.nn.sigmoid(jnp.sum(logits * hot[f, 1], axis=1, keepdims=True))
        weights = mask[f, 0].astype(jnp.float32) * (s0 / (s0 + s1)) + mask[f, 1].astype(jnp.float32) * (s1 / (s0 + s1))
        high = weights.astype(jnp.bfloat16)
        gates[f, 0] = high
        gates[f, 1] = (weights - high.astype(jnp.float32)).astype(jnp.bfloat16)

    def combine(f, j):
        loop(1, columns, lambda i: back_arrived(f, lax.rem(my_e + i, columns), j))
        results = jnp.concatenate([back[f, e, :, span(j)] for e in range(columns)], axis=0)
        return (jnp.dot(gates[f, 0], results, preferred_element_type=jnp.float32)
                + jnp.dot(gates[f, 1], results, preferred_element_type=jnp.float32))

    def sum_route(d, q):
        left = jnp.logical_xor(2 * my_f >= members, q == 1)
        f = jnp.where(left, members - 1 - d, d)
        active = jnp.where(left, my_f > f, my_f < f)
        outer = jnp.where(left, my_f < members - 1, my_f > 0)
        to = jnp.where(left, my_f - 1, my_f + 1)
        index = jnp.where(both(jnp.logical_not(left), to == f), members, f)
        return f, active, outer, jnp.clip(to, 0, members - 1), index

    def sum_copy(f, j, to, index):
        return copy(rs_out.at[f, :, span(j)], rs_in.at[index, :, span(j)],
                    s_send.at[f, j], s_recv.at[index, j], dev(my_e, to))

    def sum_arrived(index, j):
        at = rs_in.at[index, :, span(j)]
        copy(at, at, s_send.at[0, j], s_recv.at[index, j], dev(my_e, my_f)).wait_recv()

    def sum_step(d, i):
        j, q = lax.div(i, 2), lax.rem(i, 2)
        f, active, outer, to, index = sum_route(d, q)

        @pl.when(active)
        def _():
            total[...] = combine(f, j)

            @pl.when(outer)
            def _():
                sum_arrived(f, j)
                total[...] += rs_in[f, :, span(j)].astype(jnp.float32)

            rs_out[f, :, span(j)] = total[...].astype(jnp.bfloat16)
            sum_copy(f, j, to, index).start()

    shift = max(members - 3, 0)

    def slot(t):
        k, j = lax.div(t, chunks), lax.rem(t, chunks)

        @pl.when(k < members - 1)
        def _():
            t_step(k + 1, j)

        @pl.when(t == (members - 1) * chunks)
        def _():
            loop(0, chunks, lambda i: box(my_f, i))

        @pl.when(both(j == 0, both(k >= 1, k <= members)))
        def _():
            expert(group_of(lax.rem(k, members)))

        @pl.when(both(k > shift, k < members + shift))
        def _():
            loop(2 * j, 2 * j + 2, lambda i: sum_step(k - shift, i))

    loop(0, chunks * max(members + shift, members + 1), slot)

    def finish_own(j):
        total[...] = resid[:, span(j)].astype(jnp.float32) + combine(my_f, j)

        @pl.when(my_f < members - 1)
        def _():
            sum_arrived(my_f, j)
            total[...] += rs_in[my_f, :, span(j)].astype(jnp.float32)

        @pl.when(my_f > 0)
        def _():
            sum_arrived(members, j)
            total[...] += rs_in[members, :, span(j)].astype(jnp.float32)

        out[:, span(j)] = total[...].astype(jnp.bfloat16)

    loop(0, chunks, finish_own)

    def drain(j):
        w_start(j, True)
        t_start(j, True)
        loop(1, members, lambda s: w_step(s, j, True))
        loop(1, members, lambda d: t_step(d, j, True))
        for r in range(1, lines):
            part_copy(r, j).wait_send()

        def sums(i):
            f, active, outer, to, index = sum_route(lax.div(i, 2) + 1, lax.rem(i, 2))

            @pl.when(active)
            def _():
                sum_copy(f, j, to, index).wait_send()

        loop(0, 2 * (members - 1), sums)

    loop(0, chunks, drain)
    id_start(True)
    for r in range(1, lines):
        ctx_copy(r).wait_send()

    def drain_boxes(i):
        f, e = lax.div(i, columns), lax.rem(i, columns)

        @pl.when(e != my_e)
        def _():
            copy(outb.at[f, e], inb.at[f, my_e], b_send.at[f, e], b_recv.at[f, my_e], dev(e, my_f)).wait_send()
            copy(part.at[f, e], back.at[f, my_e], r_send.at[f, e], r_recv.at[f, my_e, 0], dev(e, my_f)).wait_send()

    loop(0, members * columns, drain_boxes)


def on_device(tokens, context, out_proj, norm_gain, router, expert_ids, w_gate_up, w_down):
    rows, width = tokens.shape
    columns = lax.axis_size("expert")
    members = lax.axis_size("fsdp")
    n = columns * members
    experts = n // 2
    lines = columns // 2
    cap = 5 * rows // (2 * experts)
    slots = -(-cap // 8) * 8
    units = w_down.shape[1]
    k_rows = out_proj.shape[0]
    col = min(512, width)
    chunks = width // col
    others = max(lines - 1, 1)
    vmem = pl.BlockSpec(memory_space=pltpu.VMEM)
    far = pl.BlockSpec(memory_space=pl.ANY)
    bf = jnp.bfloat16
    dma = pltpu.SemaphoreType.DMA
    boxes = pltpu.VMEM((members, columns, slots, width), bf)
    marks = pltpu.VMEM((members, 2, rows, columns * slots), bf)
    call = pl.pallas_call(
        functools.partial(block_kernel, columns, members, slots, col),
        out_shape=jax.ShapeDtypeStruct((rows, width), bf),
        in_specs=[vmem] * 6 + [far] * 2,
        out_specs=vmem,
        scratch_shapes=[
            pltpu.VMEM((2 * members * k_rows, width), bf),
            pltpu.VMEM((lines, rows, 2 * members * k_rows), bf),
            pltpu.VMEM((rows, width), jnp.float32),
            pltpu.VMEM((others, rows, width), bf),
            pltpu.VMEM((others, rows, width), bf),
            pltpu.VMEM((2, units, width), bf),
            pltpu.VMEM((units, width), bf),
            pltpu.VMEM((rows, width), bf),
            pltpu.VMEM((members, 2, rows), jnp.int32),
            pltpu.VMEM((members, 2, rows, experts), jnp.float32),
            marks,
            marks,
            pltpu.VMEM((members, rows, width), bf),
            boxes, boxes,
            pltpu.VMEM((columns * slots, units), bf),
            boxes, boxes,
            pltpu.VMEM((rows, col), jnp.float32),
            pltpu.VMEM((members, rows, width), bf),
            pltpu.VMEM((members + 1, rows, width), bf),
            dma((2,)), dma((members, chunks, 3)), dma((2, members, chunks)),
            dma((members, 2)), dma((members,)), dma((lines,)), dma((lines,)),
            dma((others, chunks)), dma((others, chunks)),
            dma((members, chunks, 2)), dma((members, chunks)),
            dma((members, columns)), dma((members, columns)),
            dma((members, columns)), dma((members, columns, chunks)),
            dma((members, chunks)), dma((members + 1, chunks)),
        ],
        compiler_params=pltpu.CompilerParams(
            collective_id=0, has_side_effects=True, vmem_limit_bytes=VMEM_GRANT),
    )
    return call(tokens, context, out_proj, norm_gain.reshape(1, width), router.T, expert_ids.T, w_gate_up, w_down)


def solution(mesh):
    group = ("sweep", "expert", "fsdp")
    return jax.shard_map(
        on_device,
        mesh=mesh,
        in_specs=(
            P(group, None), P(group, None), P(group, None), P("sweep"), P("sweep", None),
            P(group, None), P(group, None, None, None), P(group, None, None),
        ),
        out_specs=P(group, None),
        check_vma=False,
    )
```

time: 159 us -> 145 us (0.912)
  Pallas kernels: 156 us -> 143 us
    pallas_call x1, Pallas kernels: 156 us -> 143 us  [on_device(): call(tokens, context, out_proj, norm_gain.reshape(1, width), router.T, ex...]
where the time goes in v1:
time: 145 us
  Pallas kernels  143 us (99%)
  local copies, waits for them, and re-layouts  1.88 us (1%)
    pallas_call x1, Pallas kernels, on_device(): call(tokens, context, out_proj, norm_gain.reshape(1, width), router.T, ex...  143 us

profile of v1, /device:TPU:0, one launch (start us, length us, event | category | flops | bytes accessed | tf_op | source)
XLA Modules:
  0.0 144.8 jit_solution(2476718123968332787)
XLA Ops:
  0.0 142.9 %shard_map.82 = bf16[128,2048]{1,0:T(8,128)(2,1)} custom-call(bf16[128,2048]{1,0:T(8,128)(2,1)} %tok.1, bf16[128,2048]{1,0:T(8,128)(2,1)} %ctx.1, bf16[128,2048]{1,0:T(8,128)(2,1)} %wout.1, f32[1,2048]{1,0:T(1,128)} %bitcast.4, bf16[8,2048]{1,0:T(8,128)(2,1)} %bitcast.3, s32[2,128]{1,0:T(2,128)} %bitcast.5, bf16[1,2,704,2048]{3,2,1,0:T(8,128)(2,1)} %gu_hbm.1, ...), custom_call_target="tpu_custom_call" | custom-call | tf_op jit(solution)/shard_map/pallas_call | solution.py:477
  142.9 1.9 %copy.10 = bf16[128,2048]{1,0:T(8,128)(2,1)} copy(bf16[128,2048]{1,0:T(8,128)(2,1)} %shard_map.82) | data formatting | bytes 1048576

commit v2 on v1

--- a/solution.py
+++ b/solution.py
@@ -329,8 +329,7 @@
         at = rs_in.at[index, :, span(j)]
         copy(at, at, s_send.at[0, j], s_recv.at[index, j], dev(my_e, my_f)).wait_recv()
 
-    def sum_step(d, i):
-        j, q = lax.div(i, 2), lax.rem(i, 2)
+    def sum_step(d, j, q):
         f, active, outer, to, index = sum_route(d, q)
 
         @pl.when(active)
@@ -345,10 +344,24 @@
             rs_out[f, :, span(j)] = total[...].astype(jnp.bfloat16)
             sum_copy(f, j, to, index).start()
 
+    def sum_steps(d):
+        def one(i):
+            @pl.when(i < chunks)
+            def _():
+                sum_step(d, i, 0)
+
+            @pl.when(i > 0)
+            def _():
+                sum_step(d, i - 1, 1)
+
+        loop(0, chunks + 1, one)
+
     shift = max(members - 3, 0)
+    at_end = jnp.logical_or(my_f == 0, my_f == members - 1)
 
     def slot(t):
         k, j = lax.div(t, chunks), lax.rem(t, chunks)
+        summing = both(k > shift, k < members + shift)
 
         @pl.when(k < members - 1)
         def _():
@@ -358,13 +371,17 @@
         def _():
             loop(0, chunks, lambda i: box(my_f, i))
 
+        @pl.when(both(summing, both(at_end, j == 0)))
+        def _():
+            sum_steps(k - shift)
+
         @pl.when(both(j == 0, both(k >= 1, k <= members)))
         def _():
             expert(group_of(lax.rem(k, members)))
 
-        @pl.when(both(k > shift, k < members + shift))
-        def _():
-            loop(2 * j, 2 * j + 2, lambda i: sum_step(k - shift, i))
+        @pl.when(both(summing, both(jnp.logical_not(at_end), j == 1)))
+        def _():
+            sum_steps(k - shift)
 
     loop(0, chunks * max(members + shift, members + 1), slot)
 

time: 145 us -> 132 us (0.910)
  Pallas kernels: 143 us -> 129 us
    pallas_call x1, Pallas kernels: 143 us -> 129 us  [on_device(): call(tokens, context, out_proj, norm_gain.reshape(1, width), router.T, ex...]
where the time goes in v2:
time: 132 us; the launch traced here: 131 us
  Pallas kernels  129 us (98%)
  local copies, waits for them, and re-layouts  1.88 us (1%)
    pallas_call x1, Pallas kernels, on_device(): call(tokens, context, out_proj, norm_gain.reshape(1, width), router.T, ex...  129 us

profile of v2, /device:TPU:0, one launch (start us, length us, event | category | flops | bytes accessed | tf_op | source)
XLA Modules:
  0.0 131.4 jit_solution(16236321848619373150)
XLA Ops:
  0.0 129.5 %shard_map.82 = bf16[128,2048]{1,0:T(8,128)(2,1)} custom-call(bf16[128,2048]{1,0:T(8,128)(2,1)} %tok.1, bf16[128,2048]{1,0:T(8,128)(2,1)} %ctx.1, bf16[128,2048]{1,0:T(8,128)(2,1)} %wout.1, f32[1,2048]{1,0:T(1,128)} %bitcast.4, bf16[8,2048]{1,0:T(8,128)(2,1)} %bitcast.3, s32[2,128]{1,0:T(2,128)} %bitcast.5, bf16[1,2,704,2048]{3,2,1,0:T(8,128)(2,1)} %gu_hbm.1, ...), custom_call_target="tpu_custom_call" | custom-call | tf_op jit(solution)/shard_map/pallas_call | solution.py:494
  129.5 1.9 %copy.10 = bf16[128,2048]{1,0:T(8,128)(2,1)} copy(bf16[128,2048]{1,0:T(8,128)(2,1)} %shard_map.82) | data formatting | bytes 1048576

commit v3 on v2

--- a/solution.py
+++ b/solution.py
@@ -27,9 +27,9 @@
     tok, ctx, wout, gain, router, ids, gu_hbm, dn_hbm,
     out,
     gath, ctxs, acc, pout, pin, gu, dn, resid,
-    idsb, hot, mask, gates, tokb, outb, inb, hid, part, back, total, rs_out, rs_in,
+    idsb, hot, mask, gates, tokb, outb, inb, hid, part, back, given, total, rs_out, rs_in,
     load_sem, w_send, w_recv, id_send, id_recv, c_send, c_recv, p_send, p_recv,
-    t_send, t_recv, b_send, b_recv, r_send, r_recv, s_send, s_recv,
+    t_send, t_recv, b_send, b_recv, r_send, r_recv, g_send, g_recv, s_send, s_recv,
 ):
     lines = columns // 2
     pairs = members // 2
@@ -43,6 +43,7 @@
     my_y, my_c = lax.div(my_e, 2), lax.rem(my_e, 2)
     my_p = lax.div(my_f, 2)
     other = my_y * 2 + 1 - my_c
+    half_f = my_f + 1 - 2 * lax.rem(my_f, 2)
 
     def dev(e, f):
         return {"expert": e, "fsdp": f}
@@ -155,16 +156,13 @@
     loop(0, chunks, lambda j: gath.__setitem__((place(my_c, my_f), span(j)), wout[:, span(j)]))
     idsb[my_f] = ids[...]
     ctxs[0] = ctx[:, pl.ds(pl.multiple_of(my_y * depth, depth), depth)]
-    loop(0, (members - 2) * chunks, lambda i: w_step(1 + lax.div(i, chunks), lax.rem(i, chunks)))
-    for r in range(1, lines):
-        ctx_copy(r).wait_recv()
+    inner = jnp.where(2 * my_f >= members, -1, 1)
 
     def group_of(k):
         m = jnp.minimum(my_f, members - 1 - my_f)
         half = lax.div(k + 1, 2)
-        near = jnp.where(lax.rem(k, 2) == 1, my_f - half, my_f + half)
-        far = jnp.where(my_f > m, my_f - (k - m), my_f + (k - m))
-        return jnp.where(k <= 2 * m, near, far)
+        near = jnp.where(lax.rem(k, 2) == 1, my_f + inner * half, my_f - inner * half)
+        return jnp.where(k <= 2 * m, near, my_f + inner * (k - m))
 
     def make_masks(f):
         diagonal = jnp.where(
@@ -197,9 +195,6 @@
                     p_send.at[r - 1, j], p_recv.at[lines - r - 1, j], dev(line * 2 + my_c, my_f))
 
     def project(j):
-        loop(lax.div(j * members, chunks), lax.div((j + 1) * members, chunks),
-             lambda k: make_masks(group_of(k)))
-        w_step(members - 1, j)
         loop(0, members, lambda f: w_arrived(1 - my_c, f, j))
         mixed = jnp.dot(ctxs[...].reshape(lines * rows, depth), gath[:, span(j)],
                         preferred_element_type=jnp.float32)
@@ -208,7 +203,28 @@
             part_copy(r, j).start()
         acc[:, span(j)] = mixed[:rows] + tok[:, span(j)].astype(jnp.float32)
 
-    loop(0, chunks, project)
+    farthest = jnp.maximum(my_f, members - 1 - my_f)
+
+    def gather(i):
+        s, j = 1 + lax.div(i, chunks), lax.rem(i, chunks)
+
+        @pl.when(s == farthest)
+        def _():
+            @pl.when(j == 0)
+            def _():
+                for r in range(1, lines):
+                    ctx_copy(r).wait_recv()
+
+            loop(lax.div(j * members, chunks), lax.div((j + 1) * members, chunks),
+                 lambda k: make_masks(group_of(k)))
+
+        w_step(s, j)
+
+        @pl.when(s == farthest)
+        def _():
+            project(j)
+
+    loop(0, (members - 1) * chunks, gather)
 
     if lines > 1:
         def add_parts(j):
@@ -249,24 +265,24 @@
         loop(1, columns, lambda i: box_copy(f, lax.rem(my_e + i, columns), j).start())
         inb[f, my_e, :, span(j)] = outb[f, my_e, :, span(j)]
 
-    def t_step(d, j, finish=False):
-        for way, sign in ((0, 1), (1, -1)):
-            fb, to = my_f - sign * d, my_f + sign
-
-            @pl.when(inside(fb, members))
-            def _():
-                if not finish:
-                    t_copy(fb, j, way, dev(my_e, my_f)).wait_recv()
-
-                @pl.when(inside(to, members))
-                def _():
-                    onward = t_copy(fb, j, way, dev(my_e, to))
-                    onward.wait_send() if finish else onward.start()
-
-                if not finish:
-                    box(fb, j)
+    def t_step(k, j, finish=False):
+        f = group_of(k)
+        step = jnp.where(f < my_f, 1, -1)
+        to = my_f + step
+        onward = t_copy(f, j, 0, dev(my_e, jnp.clip(to, 0, members - 1)))
+        if not finish:
+            onward.wait_recv()
+
+        @pl.when(inside(to, members))
+        def _():
+            onward.wait_send() if finish else onward.start()
+
+        if not finish:
+            box(f, j)
 
     loop(0, chunks, lambda j: t_start(j, False))
+    nothing = jnp.zeros((slots, width), jnp.bfloat16)
+    loop(2, columns, lambda i: back.__setitem__((half_f, lax.rem(my_y * 2 + i, columns)), nothing))
     load_gu.wait()
     load_dn.wait()
 
@@ -277,6 +293,11 @@
     def back_arrived(f, e, j):
         copy(part.at[f, e, :, span(j)], back.at[f, e, :, span(j)],
              r_send.at[f, e], r_recv.at[f, e, j], dev(e, my_f)).wait_recv()
+
+
+    def give(e, j):
+        return copy(part.at[half_f, e, :, span(j)], given.at[e, :, span(j)],
+                    g_send.at[e, j], g_recv.at[e, j], dev(my_e, half_f))
 
     def expert(f):
         def boxes_arrived(i):
@@ -293,8 +314,27 @@
             piece = jnp.dot(hid[...], dn[:, span(j)], preferred_element_type=jnp.float32).astype(jnp.bfloat16)
             for e in range(columns):
                 part[f, e, :, span(j)] = piece[e * slots:(e + 1) * slots]
-            loop(1, columns, lambda i: back_copy(f, lax.rem(my_e + i, columns), j).start())
+            back_copy(f, other, j).start()
             back[f, my_e, :, span(j)] = part[f, my_e, :, span(j)]
+
+            def far_line(i):
+                e = lax.rem(my_y * 2 + i, columns)
+
+                @pl.when(f == half_f)
+                def _():
+                    give(e, j).start()
+
+                @pl.when(f == my_f)
+                def _():
+                    give(e, j).wait_recv()
+                    part[f, e, :, span(j)] = (part[f, e, :, span(j)].astype(jnp.float32)
+                                              + given[e, :, span(j)].astype(jnp.float32)).astype(jnp.bfloat16)
+
+                @pl.when(f != half_f)
+                def _():
+                    back_copy(f, e, j).start()
+
+            loop(2, columns, far_line)
 
         loop(0, chunks, down)
 
@@ -307,7 +347,12 @@
         gates[f, 1] = (weights - high.astype(jnp.float32)).astype(jnp.bfloat16)
 
     def combine(f, j):
-        loop(1, columns, lambda i: back_arrived(f, lax.rem(my_e + i, columns), j))
+        back_arrived(f, other, j)
+
+        @pl.when(f != half_f)
+        def _():
+            loop(2, columns, lambda i: back_arrived(f, lax.rem(my_y * 2 + i, columns), j))
+
         results = jnp.concatenate([back[f, e, :, span(j)] for e in range(columns)], axis=0)
         return (jnp.dot(gates[f, 0], results, preferred_element_type=jnp.float32)
                 + jnp.dot(gates[f, 1], results, preferred_element_type=jnp.float32))
@@ -375,7 +420,9 @@
         def _():
             sum_steps(k - shift)
 
-        @pl.when(both(j == 0, both(k >= 1, k <= members)))
+        turn = jnp.where(both(k == members - 2, jnp.logical_not(at_end)), chunks - 1, 0)
+
+        @pl.when(both(j == turn, both(k >= 1, k <= members)))
         def _():
             expert(group_of(lax.rem(k, members)))
 
@@ -430,9 +477,13 @@
         @pl.when(e != my_e)
         def _():
             copy(outb.at[f, e], inb.at[f, my_e], b_send.at[f, e], b_recv.at[f, my_e], dev(e, my_f)).wait_send()
-            copy(part.at[f, e], back.at[f, my_e], r_send.at[f, e], r_recv.at[f, my_e, 0], dev(e, my_f)).wait_send()
+
+            @pl.when(jnp.logical_or(f != half_f, lax.div(e, 2) == my_y))
+            def _():
+                copy(part.at[f, e], back.at[f, my_e], r_send.at[f, e], r_recv.at[f, my_e, 0], dev(e, my_f)).wait_send()
 
     loop(0, members * columns, drain_boxes)
+    loop(2, columns, lambda i: loop(0, chunks, lambda j: give(lax.rem(my_y * 2 + i, columns), j).wait_send()))
 
 
 def on_device(tokens, context, out_proj, norm_gain, router, expert_ids, w_gate_up, w_down):
@@ -477,6 +528,7 @@
             boxes, boxes,
             pltpu.VMEM((columns * slots, units), bf),
             boxes, boxes,
+            pltpu.VMEM((columns, slots, width), bf),
             pltpu.VMEM((rows, col), jnp.float32),
             pltpu.VMEM((members, rows, width), bf),
             pltpu.VMEM((members + 1, rows, width), bf),
@@ -486,6 +538,7 @@
             dma((members, chunks, 2)), dma((members, chunks)),
             dma((members, columns)), dma((members, columns)),
             dma((members, columns)), dma((members, columns, chunks)),
+            dma((columns, chunks)), dma((columns, chunks)),
             dma((members, chunks)), dma((members + 1, chunks)),
         ],
         compiler_params=pltpu.CompilerParams(

time: 132 us -> 126 us (0.955)
  Pallas kernels: 129 us -> 124 us
    pallas_call x1, Pallas kernels: 129 us -> 124 us  [on_device(): call(tokens, context, out_proj, norm_gain.reshape(1, width), router.T, ex...]
where the time goes in v3:
time: 126 us
  Pallas kernels  124 us (98%)
  local copies, waits for them, and re-layouts  1.88 us (1%)
    pallas_call x1, Pallas kernels, on_device(): call(tokens, context, out_proj, norm_gain.reshape(1, width), router.T, ex...  124 us

profile of v3, /device:TPU:0, one launch (start us, length us, event | category | flops | bytes accessed | tf_op | source)
XLA Modules:
  0.0 126.0 jit_solution(3510214036710061290)
XLA Ops:
  0.0 124.1 %shard_map.82 = bf16[128,2048]{1,0:T(8,128)(2,1)} custom-call(bf16[128,2048]{1,0:T(8,128)(2,1)} %tok.1, bf16[128,2048]{1,0:T(8,128)(2,1)} %ctx.1, bf16[128,2048]{1,0:T(8,128)(2,1)} %wout.1, f32[1,2048]{1,0:T(1,128)} %bitcast.4, bf16[8,2048]{1,0:T(8,128)(2,1)} %bitcast.3, s32[2,128]{1,0:T(2,128)} %bitcast.5, bf16[1,2,704,2048]{3,2,1,0:T(8,128)(2,1)} %gu_hbm.1, ...), custom_call_target="tpu_custom_call" | custom-call | tf_op jit(solution)/shard_map/pallas_call | solution.py:547
  124.1 1.9 %copy.10 = bf16[128,2048]{1,0:T(8,128)(2,1)} copy(bf16[128,2048]{1,0:T(8,128)(2,1)} %shard_map.82) | data formatting | bytes 1048576

commit v4 on v3

--- a/solution.py
+++ b/solution.py
@@ -24,18 +24,18 @@
 
 def block_kernel(
     columns, members, slots, col,
-    tok, ctx, wout, gain, router, ids, gu_hbm, dn_hbm,
+    tok_hbm, ctx_hbm, wout_hbm, gain_hbm, router_hbm, ids_hbm, gu_hbm, dn_hbm,
     out,
-    gath, ctxs, acc, pout, pin, gu, dn, resid,
+    tok, ctx, gain, router, gath, ctxs, acc, pout, pin, gu, dn, resid,
     idsb, hot, mask, gates, tokb, outb, inb, hid, part, back, given, total, rs_out, rs_in,
-    load_sem, w_send, w_recv, id_send, id_recv, c_send, c_recv, p_send, p_recv,
+    load_sem, out_sem, w_send, w_recv, id_send, id_recv, c_send, c_recv, p_send, p_recv,
     t_send, t_recv, b_send, b_recv, r_send, r_recv, g_send, g_recv, s_send, s_recv,
 ):
     lines = columns // 2
     pairs = members // 2
     experts = columns * pairs
     rows, width = tok.shape
-    k_rows = wout.shape[0]
+    k_rows = wout_hbm.shape[0]
     depth = 2 * members * k_rows
     chunks = width // col
     my_e = lax.axis_index("expert")
@@ -66,6 +66,15 @@
     load_gu = pltpu.make_async_copy(gu_hbm.at[0], gu, load_sem.at[0])
     load_dn = pltpu.make_async_copy(dn_hbm.at[0], dn, load_sem.at[1])
 
+    line_part = pl.ds(pl.multiple_of(my_y * depth, depth), depth)
+    mine_at = pl.ds(pl.multiple_of((my_c * members + my_f) * k_rows, k_rows), k_rows)
+    loads = [
+        pltpu.make_async_copy(src, dst, load_sem.at[2 + i]) for i, (src, dst) in enumerate((
+            (wout_hbm, gath.at[mine_at]), (ids_hbm, idsb.at[my_f]), (ctx_hbm, ctx),
+            (ctx_hbm.at[:, line_part], ctxs.at[0]), (tok_hbm, tok), (gain_hbm, gain), (router_hbm, router)))]
+    for load in loads:
+        load.start()
+
     barrier = pltpu.get_barrier_semaphore()
 
     def greet(e, f):
@@ -80,20 +89,23 @@
     beside = jnp.where(my_f > 0, 1, 0) + jnp.where(my_f < members - 1, 1, 0)
     pl.semaphore_wait(barrier, columns - 1 + beside)
 
+    for load in loads[:3]:
+        load.wait()
+
     def place(c, f):
         return pl.ds(pl.multiple_of((c * members + f) * k_rows, k_rows), k_rows)
 
-    def w_copy(f, j, way, target, own=False):
+    def w_copy(f, j, way, target):
         at = gath.at[place(my_c, f), span(j)]
-        return copy(wout.at[:, span(j)] if own else at, at,
+        return copy(at, at,
                     w_send.at[f, j, way], w_recv.at[my_c, f, j], target)
 
     def w_arrived(c, f, j):
         at = gath.at[place(c, f), span(j)]
         copy(at, at, w_send.at[f, j, 0], w_recv.at[c, f, j], dev(other, my_f)).wait_recv()
 
-    def id_copy(f, way, target, own=False):
-        return copy(ids if own else idsb.at[f], idsb.at[f], id_send.at[f, way], id_recv.at[f], target)
+    def id_copy(f, way, target):
+        return copy(idsb.at[f], idsb.at[f], id_send.at[f, way], id_recv.at[f], target)
 
     def ctx_copy(r):
         line = lax.rem(my_y + r, lines)
@@ -107,9 +119,9 @@
 
             @pl.when(inside(to, members))
             def _():
-                mine = w_copy(my_f, j, way, dev(my_e, to), True)
+                mine = w_copy(my_f, j, way, dev(my_e, to))
                 mine.wait_send() if finish else mine.start()
-        mine = w_copy(my_f, j, 2, dev(other, my_f), True)
+        mine = w_copy(my_f, j, 2, dev(other, my_f))
         mine.wait_send() if finish else mine.start()
 
     def id_start(finish):
@@ -118,7 +130,7 @@
 
             @pl.when(inside(to, members))
             def _():
-                mine = id_copy(my_f, way, dev(my_e, to), True)
+                mine = id_copy(my_f, way, dev(my_e, to))
                 mine.wait_send() if finish else mine.start()
 
     def w_step(s, j, finish=False):
@@ -153,10 +165,11 @@
         ctx_copy(r).start()
     load_gu.start()
     load_dn.start()
-    loop(0, chunks, lambda j: gath.__setitem__((place(my_c, my_f), span(j)), wout[:, span(j)]))
-    idsb[my_f] = ids[...]
-    ctxs[0] = ctx[:, pl.ds(pl.multiple_of(my_y * depth, depth), depth)]
+    for load in loads[3:]:
+        load.wait()
+
     inner = jnp.where(2 * my_f >= members, -1, 1)
+
 
     def group_of(k):
         m = jnp.minimum(my_f, members - 1 - my_f)
@@ -416,21 +429,27 @@
         def _():
             loop(0, chunks, lambda i: box(my_f, i))
 
-        @pl.when(both(summing, both(at_end, j == 0)))
+        early = both(k == 1, j == 1)
+        usual = both(j == 0, both(k > shift + 1, k < members + shift))
+
+        @pl.when(both(at_end, jnp.logical_or(early, usual)))
+        def _():
+            sum_steps(jnp.where(early, 1, k - shift))
+
+        turn = jnp.where(both(k == members - 2, jnp.logical_not(at_end)), chunks - 1, 0)
+
+        @pl.when(both(j == turn, both(k >= 1, k <= members)))
+        def _():
+            expert(group_of(lax.rem(k, members)))
+
+        @pl.when(both(summing, both(jnp.logical_not(at_end), j == 1)))
         def _():
             sum_steps(k - shift)
 
-        turn = jnp.where(both(k == members - 2, jnp.logical_not(at_end)), chunks - 1, 0)
-
-        @pl.when(both(j == turn, both(k >= 1, k <= members)))
-        def _():
-            expert(group_of(lax.rem(k, members)))
-
-        @pl.when(both(summing, both(jnp.logical_not(at_end), j == 1)))
-        def _():
-            sum_steps(k - shift)
-
     loop(0, chunks * max(members + shift, members + 1), slot)
+
+    def out_copy(j):
+        return pltpu.make_async_copy(tok.at[:, span(j)], out.at[:, span(j)], out_sem.at[j])
 
     def finish_own(j):
         total[...] = resid[:, span(j)].astype(jnp.float32) + combine(my_f, j)
@@ -446,8 +465,6 @@
             total[...] += rs_in[members, :, span(j)].astype(jnp.float32)
 
         out[:, span(j)] = total[...].astype(jnp.bfloat16)
-
-    loop(0, chunks, finish_own)
 
     def drain(j):
         w_start(j, True)
@@ -457,15 +474,6 @@
         for r in range(1, lines):
             part_copy(r, j).wait_send()
 
-        def sums(i):
-            f, active, outer, to, index = sum_route(lax.div(i, 2) + 1, lax.rem(i, 2))
-
-            @pl.when(active)
-            def _():
-                sum_copy(f, j, to, index).wait_send()
-
-        loop(0, 2 * (members - 1), sums)
-
     loop(0, chunks, drain)
     id_start(True)
     for r in range(1, lines):
@@ -484,6 +492,17 @@
 
     loop(0, members * columns, drain_boxes)
     loop(2, columns, lambda i: loop(0, chunks, lambda j: give(lax.rem(my_y * 2 + i, columns), j).wait_send()))
+
+    loop(0, chunks, finish_own)
+
+    def sums(i):
+        f, active, outer, to, index = sum_route(lax.div(i, 2) + 1, lax.rem(i, 2))
+
+        @pl.when(active)
+        def _():
+            loop(0, chunks, lambda j: sum_copy(f, j, to, index).wait_send())
+
+    loop(0, 2 * (members - 1), sums)
 
 
 def on_device(tokens, context, out_proj, norm_gain, router, expert_ids, w_gate_up, w_down):
@@ -500,7 +519,6 @@
     col = min(512, width)
     chunks = width // col
     others = max(lines - 1, 1)
-    vmem = pl.BlockSpec(memory_space=pltpu.VMEM)
     far = pl.BlockSpec(memory_space=pl.ANY)
     bf = jnp.bfloat16
     dma = pltpu.SemaphoreType.DMA
@@ -508,10 +526,14 @@
     marks = pltpu.VMEM((members, 2, rows, columns * slots), bf)
     call = pl.pallas_call(
         functools.partial(block_kernel, columns, members, slots, col),
-        out_shape=jax.ShapeDtypeStruct((rows, width), bf),
-        in_specs=[vmem] * 6 + [far] * 2,
-        out_specs=vmem,
+        out_shape=pltpu.VMEM((rows, width), bf),
+        in_specs=[far] * 8,
+        out_specs=pl.BlockSpec(memory_space=pltpu.VMEM),
         scratch_shapes=[
+            pltpu.VMEM((rows, width), bf),
+            pltpu.VMEM((rows, columns // 2 * 2 * members * k_rows), bf),
+            pltpu.VMEM((1, width), jnp.float32),
+            pltpu.VMEM((experts, width), bf),
             pltpu.VMEM((2 * members * k_rows, width), bf),
             pltpu.VMEM((lines, rows, 2 * members * k_rows), bf),
             pltpu.VMEM((rows, width), jnp.float32),
@@ -532,7 +554,7 @@
             pltpu.VMEM((rows, col), jnp.float32),
             pltpu.VMEM((members, rows, width), bf),
             pltpu.VMEM((members + 1, rows, width), bf),
-            dma((2,)), dma((members, chunks, 3)), dma((2, members, chunks)),
+            dma((9,)), dma((chunks,)), dma((members, chunks, 3)), dma((2, members, chunks)),
             dma((members, 2)), dma((members,)), dma((lines,)), dma((lines,)),
             dma((others, chunks)), dma((others, chunks)),
             dma((members, chunks, 2)), dma((members, chunks)),

time: 126 us -> 122 us (0.968)
  Pallas kernels: 124 us -> 121 us
    pallas_call x1, Pallas kernels: 124 us -> 121 us  [on_device(): call(tokens, context, out_proj, norm_gain.reshape(1, width), router.T, ex...]
where the time goes in v4:
time: 122 us
  Pallas kernels  121 us (99%)
    pallas_call x1, Pallas kernels, on_device(): call(tokens, context, out_proj, norm_gain.reshape(1, width), router.T, ex...  121 us

profile of v4, /device:TPU:0, one launch (start us, length us, event | category | flops | bytes accessed | tf_op | source)
XLA Modules:
  0.0 121.5 jit_solution(16309476446612399293)
XLA Ops:
  0.0 120.7 %shard_map.82 = bf16[128,2048]{1,0:T(8,128)(2,1)S(1)} custom-call(bf16[128,2048]{1,0:T(8,128)(2,1)} %tok_hbm.1, bf16[128,2048]{1,0:T(8,128)(2,1)} %ctx_hbm.1, bf16[128,2048]{1,0:T(8,128)(2,1)} %wout_hbm.1, f32[1,2048]{1,0:T(1,128)} %bitcast.4, bf16[8,2048]{1,0:T(8,128)(2,1)} %bitcast.3, s32[2,128]{1,0:T(2,128)} %bitcast.5, bf16[1,2,704,2048]{3,2,1,0:T(8,128)(2,1)} %gu_hbm.1, ...), custom_call_target="tpu_custom_call" | custom-call | tf_op jit(solution)/shard_map/pallas_call | solution.py:569
  120.7 0.8 copy.10

commit v5 on v4

--- a/solution.py
+++ b/solution.py
@@ -275,7 +275,8 @@
                                 preferred_element_type=jnp.float32).astype(jnp.bfloat16)
         for e in range(columns):
             outb[f, e, :, span(j)] = boxed[e * slots:(e + 1) * slots]
-        loop(1, columns, lambda i: box_copy(f, lax.rem(my_e + i, columns), j).start())
+        loop(2, columns, lambda i: box_copy(f, lax.rem(my_y * 2 + i, columns), j).start())
+        box_copy(f, other, j).start()
         inb[f, my_e, :, span(j)] = outb[f, my_e, :, span(j)]
 
     def t_step(k, j, finish=False):
@@ -294,8 +295,6 @@
             box(f, j)
 
     loop(0, chunks, lambda j: t_start(j, False))
-    nothing = jnp.zeros((slots, width), jnp.bfloat16)
-    loop(2, columns, lambda i: back.__setitem__((half_f, lax.rem(my_y * 2 + i, columns)), nothing))
     load_gu.wait()
     load_dn.wait()
 
@@ -327,27 +326,25 @@
             piece = jnp.dot(hid[...], dn[:, span(j)], preferred_element_type=jnp.float32).astype(jnp.bfloat16)
             for e in range(columns):
                 part[f, e, :, span(j)] = piece[e * slots:(e + 1) * slots]
-            back_copy(f, other, j).start()
-            back[f, my_e, :, span(j)] = part[f, my_e, :, span(j)]
-
-            def far_line(i):
-                e = lax.rem(my_y * 2 + i, columns)
-
-                @pl.when(f == half_f)
-                def _():
-                    give(e, j).start()
-
-                @pl.when(f == my_f)
-                def _():
-                    give(e, j).wait_recv()
-                    part[f, e, :, span(j)] = (part[f, e, :, span(j)].astype(jnp.float32)
-                                              + given[e, :, span(j)].astype(jnp.float32)).astype(jnp.bfloat16)
-
-                @pl.when(f != half_f)
-                def _():
-                    back_copy(f, e, j).start()
-
-            loop(2, columns, far_line)
+
+            @pl.when(f == half_f)
+            def _():
+                loop(0, columns, lambda e: give(e, j).start())
+
+            def add_half(e):
+                give(e, j).wait_recv()
+                part[f, e, :, span(j)] = (part[f, e, :, span(j)].astype(jnp.float32)
+                                          + given[e, :, span(j)].astype(jnp.float32)).astype(jnp.bfloat16)
+
+            @pl.when(f == my_f)
+            def _():
+                loop(0, columns, add_half)
+
+            @pl.when(f != half_f)
+            def _():
+                loop(2, columns, lambda i: back_copy(f, lax.rem(my_y * 2 + i, columns), j).start())
+                back_copy(f, other, j).start()
+                back[f, my_e, :, span(j)] = part[f, my_e, :, span(j)]
 
         loop(0, chunks, down)
 
@@ -360,12 +357,7 @@
         gates[f, 1] = (weights - high.astype(jnp.float32)).astype(jnp.bfloat16)
 
     def combine(f, j):
-        back_arrived(f, other, j)
-
-        @pl.when(f != half_f)
-        def _():
-            loop(2, columns, lambda i: back_arrived(f, lax.rem(my_y * 2 + i, columns), j))
-
+        loop(1, columns, lambda i: back_arrived(f, lax.rem(my_e + i, columns), j))
         results = jnp.concatenate([back[f, e, :, span(j)] for e in range(columns)], axis=0)
         return (jnp.dot(gates[f, 0], results, preferred_element_type=jnp.float32)
                 + jnp.dot(gates[f, 1], results, preferred_element_type=jnp.float32))
@@ -373,8 +365,8 @@
     def sum_route(d, q):
         left = jnp.logical_xor(2 * my_f >= members, q == 1)
         f = jnp.where(left, members - 1 - d, d)
-        active = jnp.where(left, my_f > f, my_f < f)
         outer = jnp.where(left, my_f < members - 1, my_f > 0)
+        active = both(jnp.where(left, my_f > f, my_f < f), jnp.logical_or(f != half_f, outer))
         to = jnp.where(left, my_f - 1, my_f + 1)
         index = jnp.where(both(jnp.logical_not(left), to == f), members, f)
         return f, active, outer, jnp.clip(to, 0, members - 1), index
@@ -392,7 +384,13 @@
 
         @pl.when(active)
         def _():
-            total[...] = combine(f, j)
+            @pl.when(f != half_f)
+            def _():
+                total[...] = combine(f, j)
+
+            @pl.when(f == half_f)
+            def _():
+                total[...] = jnp.zeros_like(total)
 
             @pl.when(outer)
             def _():
@@ -425,22 +423,25 @@
         def _():
             t_step(k + 1, j)
 
-        @pl.when(t == (members - 1) * chunks)
+        @pl.when(both(t == (members - 1) * chunks, jnp.logical_not(at_end)))
         def _():
             loop(0, chunks, lambda i: box(my_f, i))
 
-        early = both(k == 1, j == 1)
         usual = both(j == 0, both(k > shift + 1, k < members + shift))
 
-        @pl.when(both(at_end, jnp.logical_or(early, usual)))
-        def _():
-            sum_steps(jnp.where(early, 1, k - shift))
+        @pl.when(both(at_end, usual))
+        def _():
+            sum_steps(k - shift)
 
         turn = jnp.where(both(k == members - 2, jnp.logical_not(at_end)), chunks - 1, 0)
 
         @pl.when(both(j == turn, both(k >= 1, k <= members)))
         def _():
             expert(group_of(lax.rem(k, members)))
+
+        @pl.when(both(t == (members - 1) * chunks, at_end))
+        def _():
+            loop(0, chunks, lambda i: box(my_f, i))
 
         @pl.when(both(summing, both(jnp.logical_not(at_end), j == 1)))
         def _():
@@ -454,12 +455,12 @@
     def finish_own(j):
         total[...] = resid[:, span(j)].astype(jnp.float32) + combine(my_f, j)
 
-        @pl.when(my_f < members - 1)
+        @pl.when(members - 1 - my_f > 1 - lax.rem(my_f, 2))
         def _():
             sum_arrived(my_f, j)
             total[...] += rs_in[my_f, :, span(j)].astype(jnp.float32)
 
-        @pl.when(my_f > 0)
+        @pl.when(my_f > lax.rem(my_f, 2))
         def _():
             sum_arrived(members, j)
             total[...] += rs_in[members, :, span(j)].astype(jnp.float32)
@@ -486,12 +487,12 @@
         def _():
             copy(outb.at[f, e], inb.at[f, my_e], b_send.at[f, e], b_recv.at[f, my_e], dev(e, my_f)).wait_send()
 
-            @pl.when(jnp.logical_or(f != half_f, lax.div(e, 2) == my_y))
+            @pl.when(f != half_f)
             def _():
                 copy(part.at[f, e], back.at[f, my_e], r_send.at[f, e], r_recv.at[f, my_e, 0], dev(e, my_f)).wait_send()
 
     loop(0, members * columns, drain_boxes)
-    loop(2, columns, lambda i: loop(0, chunks, lambda j: give(lax.rem(my_y * 2 + i, columns), j).wait_send()))
+    loop(0, columns, lambda e: loop(0, chunks, lambda j: give(e, j).wait_send()))
 
     loop(0, chunks, finish_own)
 

time: 122 us -> 120 us (0.984)
  Pallas kernels: 121 us -> 119 us
    pallas_call x1, Pallas kernels: 121 us -> 119 us  [on_device(): call(tokens, context, out_proj, norm_gain.reshape(1, width), router.T, ex...]
where the time goes in v5:
time: 120 us
  Pallas kernels  119 us (99%)
    pallas_call x1, Pallas kernels, on_device(): call(tokens, context, out_proj, norm_gain.reshape(1, width), router.T, ex...  119 us

profile of v5, /device:TPU:0, one launch (start us, length us, event | category | flops | bytes accessed | tf_op | source)
XLA Modules:
  0.0 119.6 jit_solution(11400156545546733131)
XLA Ops:
  0.0 118.8 %shard_map.82 = bf16[128,2048]{1,0:T(8,128)(2,1)S(1)} custom-call(bf16[128,2048]{1,0:T(8,128)(2,1)} %tok_hbm.1, bf16[128,2048]{1,0:T(8,128)(2,1)} %ctx_hbm.1, bf16[128,2048]{1,0:T(8,128)(2,1)} %wout_hbm.1, f32[1,2048]{1,0:T(1,128)} %bitcast.4, bf16[8,2048]{1,0:T(8,128)(2,1)} %bitcast.3, s32[2,128]{1,0:T(2,128)} %bitcast.5, bf16[1,2,704,2048]{3,2,1,0:T(8,128)(2,1)} %gu_hbm.1, ...), custom_call_target="tpu_custom_call" | custom-call | tf_op jit(solution)/shard_map/pallas_call | solution.py:570
  118.8 0.8 copy.10

commit v6 on v5

--- a/solution.py
+++ b/solution.py
@@ -433,7 +433,7 @@
         def _():
             sum_steps(k - shift)
 
-        turn = jnp.where(both(k == members - 2, jnp.logical_not(at_end)), chunks - 1, 0)
+        turn = jnp.where(k == members - 2, jnp.where(at_end, min(1, chunks - 1), chunks - 1), 0)
 
         @pl.when(both(j == turn, both(k >= 1, k <= members)))
         def _():
@@ -443,7 +443,7 @@
         def _():
             loop(0, chunks, lambda i: box(my_f, i))
 
-        @pl.when(both(summing, both(jnp.logical_not(at_end), j == 1)))
+        @pl.when(both(summing, both(jnp.logical_not(at_end), j == min(1, chunks - 1))))
         def _():
             sum_steps(k - shift)
 

time: 120 us -> 118 us (0.983)
  Pallas kernels: 119 us -> 117 us
    pallas_call x1, Pallas kernels: 119 us -> 117 us  [on_device(): call(tokens, context, out_proj, norm_gain.reshape(1, width), router.T, ex...]
where the time goes in v6:
time: 118 us
  Pallas kernels  117 us (99%)
    pallas_call x1, Pallas kernels, on_device(): call(tokens, context, out_proj, norm_gain.reshape(1, width), router.T, ex...  117 us

profile of v6, /device:TPU:0, one launch (start us, length us, event | category | flops | bytes accessed | tf_op | source)
XLA Modules:
  0.0 118.1 jit_solution(15856561499667665480)
XLA Ops:
  0.0 117.3 %shard_map.82 = bf16[128,2048]{1,0:T(8,128)(2,1)S(1)} custom-call(bf16[128,2048]{1,0:T(8,128)(2,1)} %tok_hbm.1, bf16[128,2048]{1,0:T(8,128)(2,1)} %ctx_hbm.1, bf16[128,2048]{1,0:T(8,128)(2,1)} %wout_hbm.1, f32[1,2048]{1,0:T(1,128)} %bitcast.4, bf16[8,2048]{1,0:T(8,128)(2,1)} %bitcast.3, s32[2,128]{1,0:T(2,128)} %bitcast.5, bf16[1,2,704,2048]{3,2,1,0:T(8,128)(2,1)} %gu_hbm.1, ...), custom_call_target="tpu_custom_call" | custom-call | tf_op jit(solution)/shard_map/pallas_call | solution.py:570
  117.3 0.8 copy.10
